TPU v7x, 32 devices: a whole 2x2x4 slice. The times are simulated.
32 devices in a mesh: ep: 8 (over z, y), dp: 4 (over x, core).
Axes of the slice: x: 2, y: 2, z: 4, core: 2. Of those that a mesh axis runs over, the one named last changes fastest.
Arguments:
- tokens: bfloat16 [6144, 2880], P(('ep', 'dp')), may hold values from -64 to 64
- out_grad: bfloat16 [6144, 2880], P(('ep', 'dp')), may hold values from -6 to 6
- indices: int32 [6144, 4], P(('ep', 'dp')), may hold values from 0 to 31, as said below
- expert_rows: bfloat16 [4, 32, 8, 36, 2880], P('dp', 'ep'), may hold values from -0.111328125 to 0.111328125
- router_weight: bfloat16 [2880, 32], replicated, may hold values from -1 to 1
- router_bias: float32 [32], replicated, may hold values from -3 to 3
- balance_scale: float32 [1], replicated, may hold values from 64 to 256
Outputs:
- token_grad: bfloat16 [6144, 2880], P(('ep', 'dp'))
- weight_grad: float32 [2880, 32], P('dp', 'ep')
- balance_loss: float32 [1], replicated
Inputs may be any that keep to these rules, and one draw needn't show every extreme that they name: `indices`: each row names 4 different experts. Within the 192 rows of one device no expert is named by more than 36 rows, and some expert is named by exactly 36 rows. Within the rows of one device the 4 experts of one ep index (experts j * 4 to j * 4 + 3) are named by at most 108 rows together, and those of some ep index by exactly 108. Every expert is named by some row of every device.
All inputs are finite; a program needn't handle non-finite values.
Results may differ from a plain program's by a relative error of at most 0.0014.
The roundings to bfloat16 on the way count: a program that leaves them out, or rounds other values in their place, can miss the bound.
Values may be sent and summed in bfloat16 or wider, within the bound.
No kernel may reach another device: no remote copies, remote signals or barrier semaphores. Data moves between devices by JAX's collectives and lax.ppermute only.
A program may use at most 128 MiB of HBM per device.

v0:
```python
import math
import jax
import jax.numpy as jnp
from jax import lax
from jax.sharding import PartitionSpec as P


def on_device(tokens, out_grad, indices, expert_rows, router_weight, router_bias, balance_scale):
    tok_dev = tokens.shape[0]
    chosen = indices.shape[1]
    width = tokens.shape[1]
    experts = router_weight.shape[1]
    capacity = expert_rows.shape[3]
    ep_size = lax.axis_size("ep")
    dp_size = lax.axis_size("dp")
    token_total = tok_dev * ep_size * dp_size
    expert_ids = jnp.arange(experts, dtype=jnp.int32)
    onehot = (indices[:, :, None] == expert_ids[None, None, :]).astype(jnp.float32)
    named_by = jnp.sum(onehot, axis=1)
    local_counts = jnp.sum(named_by, axis=0)
    logits = jnp.dot(tokens, router_weight, preferred_element_type=jnp.float32) + router_bias
    probability = jax.nn.softmax(logits, axis=-1)
    counts, prob_sums = lax.psum((local_counts, jnp.sum(probability, axis=0)), ("ep", "dp"))
    share_of = counts / (token_total * chosen)
    balance_loss = (experts * jnp.sum(share_of * (prob_sums / token_total))).reshape(1)
    row_ids = jnp.arange(tok_dev, dtype=jnp.int32)
    lower_mask = (row_ids[:, None] > row_ids[None, :]).astype(jnp.bfloat16)
    before = jnp.dot(lower_mask, named_by.astype(jnp.bfloat16), preferred_element_type=jnp.float32)
    slot_index = jnp.sum(onehot * before[:, None, :], axis=2).astype(jnp.int32)
    returned = lax.all_to_all(expert_rows, "ep", split_axis=2, concat_axis=1, tiled=True)
    flat_rows = returned.reshape(experts * capacity, width)
    row_index = indices * capacity + slot_index
    picked = jnp.take(flat_rows, row_index, axis=0)
    pair_dots = jnp.einsum("td,tkd->tk", out_grad, picked, preferred_element_type=jnp.float32)
    chosen_logits = jnp.take_along_axis(logits, indices, axis=1)
    mix_weight = jax.nn.softmax(chosen_logits, axis=-1)
    sel_grad = mix_weight * (pair_dots - jnp.sum(mix_weight * pair_dots, axis=1, keepdims=True))
    balance_push = balance_scale[0] * experts * share_of
    spread = probability * (
        balance_push[None, :] - jnp.sum(probability * balance_push[None, :], axis=1, keepdims=True)
    )
    logit_grad = (spread + jnp.sum(onehot * sel_grad[:, :, None], axis=1)).astype(jnp.bfloat16)
    token_grad = lax.dot_general(
        logit_grad, router_weight, (((1,), (1,)), ((), ())), preferred_element_type=jnp.float32
    ).astype(jnp.bfloat16)
    term = lax.dot_general(
        tokens, logit_grad, (((0,), (0,)), ((), ())), preferred_element_type=jnp.float32
    )
    summed = lax.psum_scatter(term, "ep", scatter_dimension=1, tiled=True)
    summed = lax.psum_scatter(summed, "dp", scatter_dimension=0, tiled=True)
    weight_grad = summed / math.sqrt(token_total)
    return (token_grad, weight_grad, balance_loss)


def solution(mesh):
    placed = (
        P(("ep", "dp"), None),
        P(("ep", "dp"), None),
        P(("ep", "dp"), None),
        P("dp", "ep", None, None, None),
        P(),
        P(),
        P(),
    )
    return jax.shard_map(
        on_device,
        mesh=mesh,
        in_specs=placed,
        out_specs=(P(("ep", "dp"), None), P("dp", "ep"), P()),
        check_vma=False,
    )
```

profile of v0, /device:TPU:0, one launch (start us, length us, event | category | flops | bytes accessed | tf_op | source)
XLA Modules:
  0.0 366.3 jit_solution(14106931418418347998)
XLA Ops:
  7.2 7.0 %copy.48 = bf16[1,4,8,36,2880]{4,3,1,0,2:T(8,128)(2,1)} copy(bf16[1,4,8,36,2880]{4,2,3,1,0:T(8,128)(2,1)} %param.10) | data formatting | bytes 13271040 | tf_op args[3]
  14.2 7.5 %all-to-all-start = ((bf16[1,4,8,36,2880]{4,3,1,0,2:T(8,128)(2,1)}), bf16[1,4,8,36,2880]{4,3,1,0,2:T(8,128)(2,1)}, u32[]{:S(2)}, u32[]{:S(2)}) async-start(bf16[1,4,8,36,2880]{4,3,1,0,2:T(8,128)(2,1)} %copy.48), calls=%async_computation | async-start | bytes 15073280 | tf_op jit(solution)/shard_map/all_to_all | solution.py:30
  21.8 0.1 fusion.5
  21.9 0.2 convert_reduce_fusion.1
  22.1 184.7 %psum.14 = f32[32]{0:T(128)S(1)} all-reduce(f32[32]{0:T(128)S(1)} %get-tuple-element.5), channel_id=1, replica_groups=mesh['ep'=8,'dp'=4] {'ep','dp'}, use_global_device_ids=true, to_apply=%region_3.0 | all-reduce | flops 32 | bytes 256 | tf_op jit(solution)/shard_map/psum | solution.py:23
  207.0 0.2 copy.47
  207.4 0.5 fusion.16
  207.9 6.3 %gather_fusion.1 = f32[768]{0:T(1024)S(1)} fusion(f32[192,32]{0,1:T(8,128)S(1)} %get-tuple-element.12, s32[768]{0:T(1024)S(1)} %reshape.51), kind=kCustom, calls=%fused_computation.1 | custom fusion | bytes 12288 | tf_op jit(solution)/shard_map/jit(take_along_axis)/gather | solution.py:35
  215.2 0.1 fusion.14
  215.4 9.3 %reshape.41 = bf16[1152,2880]{1,0:T(8,128)(2,1)} reshape(bf16[1,8,4,1,36,2880]{5,4,2,1,3,0:T(8,128)(2,1)} %bitcast.3) | data formatting | bytes 13271040 | tf_op jit(solution)/shard_map/reshape | solution.py:31
  224.7 13.1 %gather_fusion = bf16[768,2880]{1,0:T(8,128)(2,1)} fusion(bf16[1152,2880]{1,0:T(8,128)(2,1)} %reshape.41, s32[1024]{0:T(1024)S(1)} %pad_clamp_fusion), kind=kCustom, calls=%fused_computation | custom fusion | bytes 8850432 | tf_op jit(solution)/shard_map/jit(_take)/gather | solution.py:33
  237.8 7.1 %reshape.44 = bf16[192,4,2880]{2,1,0:T(4,128)(2,1)} reshape(bf16[768,2880]{1,0:T(8,128)(2,1)} %gather_fusion) | data formatting | bytes 8847360 | tf_op jit(solution)/shard_map/jit(_take)/gather | solution.py:33
  244.9 9.4 %fusion = f32[192,1,4]{2,1,0:T(1,128)S(1)} fusion(bf16[192,4,2880]{2,1,0:T(4,128)(2,1)} %reshape.44, pred[192,4]{1,0:T(8,128)(4,1)S(1)} %copy.47, bf16[192,2880,1]{1,0,2:T(8,128)(2,1)S(1)} %bitcast.30), kind=kOutput, calls=%fused_computation.2 | convolution fusion | flops 6635520 | bytes 5533440 | tf_op jit(solution)/shard_map/td,tkd->tk/dot_general | solution.py:34
  254.6 1.1 convolution_bitcast_fusion
  255.7 39.3 %psum.15 = f32[32]{0:T(128)S(1)} all-reduce(f32[32]{0:T(128)S(1)} %get-tuple-element.3), channel_id=1, replica_groups=mesh['ep'=8,'dp'=4] {'ep','dp'}, use_global_device_ids=true, to_apply=%region_14.15 | all-reduce | flops 32 | bytes 256 | tf_op jit(solution)/shard_map/psum | solution.py:23
  295.0 0.6 dynamic-slice
  296.3 0.6 multiply_reduce_fusion.1
  297.5 29.8 %all-reduce.3.cloned.1.call-done = f32[2880,32]{0,1:T(8,128)} async-done(((f32[2880,32]{0,1:T(8,128)}), f32[2880,32]{0,1:T(8,128)}) %all-reduce.3.cloned.1.call-update) | async-done | bytes 368656
  327.3 0.9 constant_dynamic-slice_fusion
  328.2 1.6 copy.52
  329.9 1.5 convolution_convert_fusion
  331.4 25.2 %reduce-scatter.4.cloned.1.call-done = f32[720,4]{1,0:T(8,128)} async-done(((f32[2880,4]{1,0:T(8,128)}), f32[720,4]{1,0:T(8,128)}) %reduce-scatter.4.cloned.1.call-update) | async-done | bytes 11536
  356.6 1.1 copy.53
  357.7 0.6 broadcast_multiply_fusion
  (36 shorter events, 1.2 us)
Async XLA Ops:
  7.2 237.8 %copy-start = (bf16[192,2880]{1,0:T(8,128)(2,1)S(1)}, bf16[192,2880]{1,0:T(8,128)(2,1)}, u32[]{:S(2)}) copy-start(bf16[192,2880]{1,0:T(8,128)(2,1)} %param.8) | copy-start | bytes 3317764
  14.2 7.5 %copy-start.3 = (s32[192,4]{0,1:T(4,128)S(1)}, s32[192,4]{0,1:T(4,128)}, u32[]{:S(2)}) copy-start(s32[192,4]{0,1:T(4,128)} %param.9) | copy-start | bytes 9220
  14.2 193.2 %copy-start.1 = (bf16[192,2880]{1,0:T(8,128)(2,1)S(1)}, bf16[192,2880]{1,0:T(8,128)(2,1)}, u32[]{:S(2)}) copy-start(bf16[192,2880]{1,0:T(8,128)(2,1)} %param.7) | copy-start | bytes 3317764
  14.2 193.2 %copy-start.2 = (bf16[2880,32]{0,1:T(8,128)(2,1)S(1)}, bf16[2880,32]{0,1:T(8,128)(2,1)}, u32[]{:S(2)}) copy-start(bf16[2880,32]{0,1:T(8,128)(2,1)} %param.11) | copy-start | bytes 552964
  14.2 193.2 %copy-start.4 = (f32[32]{0:T(128)S(1)}, f32[32]{0:T(128)}, u32[]{:S(2)}) copy-start(f32[32]{0:T(128)} %param.12) | copy-start | bytes 388
  14.2 201.1 %all-to-all-start = ((bf16[1,4,8,36,2880]{4,3,1,0,2:T(8,128)(2,1)}), bf16[1,4,8,36,2880]{4,3,1,0,2:T(8,128)(2,1)}, u32[]{:S(2)}, u32[]{:S(2)}) async-start(bf16[1,4,8,36,2880]{4,3,1,0,2:T(8,128)(2,1)} %copy.48), calls=%async_computation | async-start | bytes 15073280 | tf_op jit(solution)/shard_map/all_to_all | solution.py:30
  21.7 305.6 %all-reduce.3.cloned.1.call-start = ((), (), s32[]{:S(2)}) async-start(), calls=%async_computation.3 | async-start | bytes 753664
  244.9 50.1 %copy-start.5 = (u32[32]{0:T(128)S(1)}, u32[32]{0:T(128)}, u32[]{:S(2)}) copy-start(u32[32]{0:T(128)} %constant.70) | copy-start | bytes 388
  255.7 100.9 %reduce-scatter.4.cloned.1.call-start = ((), (), s32[]{:S(2)}) async-start(), calls=%async_computation.2 | async-start | bytes 1843200
Sparse Core Ops, SparseCore 0:
  255.8 71.4 all-reduce.2
  330.0 26.5 reduce-scatter.3
where the time goes:
time: 367 us; the launch traced here: 366 us
  blocking collectives  224 us (61%)
  waiting for transfers between devices  55.1 us (15%)
  local copies, waits for them, and re-layouts  48.1 us (13%)
  between operations  17.3 us (5%)
  matrix products  12.6 us (3%)
  starting transfers between devices  7.53 us (2%)
    psum x2, blocking collectives, on_device(): lax.psum((local_counts, jnp.sum(probability, axis=0)), ('ep', 'dp'))  224 us
    unnamed x4, waiting for transfers between devices  55.1 us
    gather x2, local copies, waits for them, and re-layouts, on_device(): picked = jnp.take(flat_rows, row_index, axis=0)  20.2 us
    unnamed x17, local copies, waits for them, and re-layouts  11.3 us
    dot_general x1, matrix products, on_device(): jnp.einsum('td,tkd->tk', out_grad, picked, preferred_element_type=jnp.flo...  9.4 us
    reshape x1, local copies, waits for them, and re-layouts, on_device(): flat_rows = returned.reshape(experts * capacity, width)  9.32 us
    all_to_all x1, starting transfers between devices, on_device(): lax.all_to_all(expert_rows, 'ep', split_axis=2, concat_axis=1, tiled=True)  7.45 us
  transfers between devices with their start and end apart: 3, of which 2 were waited for; matrix products, arithmetic and copies ran while one was open for 3% of the time, Pallas kernels for 0%

commit v1 on v0

--- a/solution.py
+++ b/solution.py
@@ -3,6 +3,11 @@
 import jax.numpy as jnp
 from jax import lax
 from jax.sharding import PartitionSpec as P
+
+
+def by_each_axis(value, axis_one, axis_two):
+    half = lax.psum(value, axis_one)
+    return lax.psum(half, axis_two)
 
 
 def on_device(tokens, out_grad, indices, expert_rows, router_weight, router_bias, balance_scale):
@@ -20,7 +25,7 @@
     local_counts = jnp.sum(named_by, axis=0)
     logits = jnp.dot(tokens, router_weight, preferred_element_type=jnp.float32) + router_bias
     probability = jax.nn.softmax(logits, axis=-1)
-    counts, prob_sums = lax.psum((local_counts, jnp.sum(probability, axis=0)), ("ep", "dp"))
+    counts, prob_sums = by_each_axis((local_counts, jnp.sum(probability, axis=0)), "dp", "ep")
     share_of = counts / (token_total * chosen)
     balance_loss = (experts * jnp.sum(share_of * (prob_sums / token_total))).reshape(1)
     row_ids = jnp.arange(tok_dev, dtype=jnp.int32)

time: 367 us -> 346 us (0.943)
  blocking collectives: 224 us -> 173 us
  waiting for transfers between devices: 55.1 us -> 85.3 us
    psum x2 -> x4, blocking collectives: 224 us -> 173 us  [the longest x2 160 us: by_each_axis(): return lax.psum(half, axis_two)]
    all_to_all x1, waiting for transfers between devices: 0.01 us -> 16.9 us  [on_device(): lax.all_to_all(expert_rows, 'ep', split_axis=2, concat_axis=1, tiled=True)]
    unnamed x4, waiting for transfers between devices: 55.1 us -> 68.4 us
  transfers between devices with their start and end apart: 3 -> 3, of which waited for: 2 -> 3; matrix products, arithmetic and copies ran while one was open for 3% -> 3% of each run, Pallas kernels for 0% -> 0%
where the time goes in v1:
time: 346 us; the launch traced here: 345 us
  blocking collectives  173 us (50%)
  waiting for transfers between devices  85.3 us (25%)
  local copies, waits for them, and re-layouts  48.1 us (14%)
  between operations  17.3 us (5%)
  matrix products  12.6 us (4%)
  starting transfers between devices  7.53 us (2%)
    psum x2, blocking collectives, by_each_axis(): return lax.psum(half, axis_two)  160 us
    unnamed x4, waiting for transfers between devices  68.4 us
    gather x2, local copies, waits for them, and re-layouts, on_device(): picked = jnp.take(flat_rows, row_index, axis=0)  20.2 us
    all_to_all x1, waiting for transfers between devices, on_device(): lax.all_to_all(expert_rows, 'ep', split_axis=2, concat_axis=1, tiled=True)  16.9 us
    psum x2, blocking collectives, by_each_axis(): half = lax.psum(value, axis_one)  12.4 us
    unnamed x17, local copies, waits for them, and re-layouts  11.3 us
    dot_general x1, matrix products, on_device(): jnp.einsum('td,tkd->tk', out_grad, picked, preferred_element_type=jnp.flo...  9.4 us
    reshape x1, local copies, waits for them, and re-layouts, on_device(): flat_rows = returned.reshape(experts * capacity, width)  9.31 us
  transfers between devices with their start and end apart: 3, of which 3 were waited for; matrix products, arithmetic and copies ran while one was open for 3% of the time, Pallas kernels for 0%

profile of v1, /device:TPU:0, one launch (start us, length us, event | category | flops | bytes accessed | tf_op | source)
XLA Modules:
  0.0 345.3 jit_solution(11753358687123654903)
XLA Ops:
  7.2 7.0 %copy.48 = bf16[1,4,8,36,2880]{4,3,1,0,2:T(8,128)(2,1)} copy(bf16[1,4,8,36,2880]{4,2,3,1,0:T(8,128)(2,1)} %param.10) | data formatting | bytes 13271040 | tf_op args[3]
  14.2 7.5 %all-to-all-start = ((bf16[1,4,8,36,2880]{4,3,1,0,2:T(8,128)(2,1)}), bf16[1,4,8,36,2880]{4,3,1,0,2:T(8,128)(2,1)}, u32[]{:S(2)}, u32[]{:S(2)}) async-start(bf16[1,4,8,36,2880]{4,3,1,0,2:T(8,128)(2,1)} %copy.48), calls=%async_computation | async-start | bytes 15073280 | tf_op jit(solution)/shard_map/all_to_all | solution.py:35
  21.9 0.2 convert_reduce_fusion.1
  22.8 0.5 fusion.16
  23.3 6.3 %gather_fusion.1 = f32[768]{0:T(1024)S(1)} fusion(f32[192,32]{0,1:T(8,128)S(1)} %get-tuple-element.12, s32[768]{0:T(1024)S(1)} %reshape.51), kind=kCustom, calls=%fused_computation.1 | custom fusion | bytes 12288 | tf_op jit(solution)/shard_map/jit(take_along_axis)/gather | solution.py:40
  30.5 6.7 %psum.28 = f32[32]{0:T(128)S(1)} all-reduce(f32[32]{0:T(128)S(1)} %get-tuple-element.5), channel_id=1, replica_groups=mesh['ep'=8,'dp'=4] {'dp'}, use_global_device_ids=true, to_apply=%region_3.0 | all-reduce | flops 32 | bytes 256 | tf_op jit(solution)/shard_map/psum | solution.py:9
  37.2 132.4 %psum.29 = f32[32]{0:T(128)S(1)} all-reduce(f32[32]{0:T(128)S(1)} %psum.28), channel_id=1, replica_groups=mesh['ep'=8,'dp'=4] {'ep'}, use_global_device_ids=true, to_apply=%region_4.0 | all-reduce | flops 32 | bytes 256 | tf_op jit(solution)/shard_map/psum | solution.py:10
  169.8 16.9 %all-to-all-done = bf16[1,4,8,36,2880]{4,3,1,0,2:T(8,128)(2,1)} async-done(((bf16[1,4,8,36,2880]{4,3,1,0,2:T(8,128)(2,1)}), bf16[1,4,8,36,2880]{4,3,1,0,2:T(8,128)(2,1)}, u32[]{:S(2)}, u32[]{:S(2)}) %all-to-all-start) | async-done | bytes 6635552 | tf_op jit(solution)/shard_map/all_to_all | solution.py:35
  186.7 9.3 %reshape.41 = bf16[1152,2880]{1,0:T(8,128)(2,1)} reshape(bf16[1,8,4,1,36,2880]{5,4,2,1,3,0:T(8,128)(2,1)} %bitcast.3) | data formatting | bytes 13271040 | tf_op jit(solution)/shard_map/reshape | solution.py:36
  196.0 13.1 %gather_fusion = bf16[768,2880]{1,0:T(8,128)(2,1)} fusion(bf16[1152,2880]{1,0:T(8,128)(2,1)} %reshape.41, s32[1024]{0:T(1024)S(1)} %pad_clamp_fusion), kind=kCustom, calls=%fused_computation | custom fusion | bytes 8850432 | tf_op jit(solution)/shard_map/jit(_take)/gather | solution.py:38
  209.1 7.1 %reshape.44 = bf16[192,4,2880]{2,1,0:T(4,128)(2,1)} reshape(bf16[768,2880]{1,0:T(8,128)(2,1)} %gather_fusion) | data formatting | bytes 8847360 | tf_op jit(solution)/shard_map/jit(_take)/gather | solution.py:38
  216.2 9.4 %fusion = f32[192,1,4]{2,1,0:T(1,128)S(1)} fusion(bf16[192,4,2880]{2,1,0:T(4,128)(2,1)} %reshape.44, pred[192,4]{1,0:T(8,128)(4,1)S(1)} %copy.47, bf16[192,2880,1]{1,0,2:T(8,128)(2,1)S(1)} %bitcast.30), kind=kOutput, calls=%fused_computation.2 | convolution fusion | flops 6635520 | bytes 5533440 | tf_op jit(solution)/shard_map/td,tkd->tk/dot_general | solution.py:39
  225.9 1.1 convolution_bitcast_fusion
  227.1 0.6 dynamic-slice
  228.3 5.7 %psum.30 = f32[32]{0:T(128)S(1)} all-reduce(f32[32]{0:T(128)S(1)} %get-tuple-element.3), channel_id=1, replica_groups=mesh['ep'=8,'dp'=4] {'dp'}, use_global_device_ids=true, to_apply=%region_15.16 | all-reduce | flops 32 | bytes 256 | tf_op jit(solution)/shard_map/psum | solution.py:9
  234.0 27.9 %psum.31 = f32[32]{0:T(128)S(1)} all-reduce(f32[32]{0:T(128)S(1)} %psum.30), channel_id=1, replica_groups=mesh['ep'=8,'dp'=4] {'ep'}, use_global_device_ids=true, to_apply=%region_16.17 | all-reduce | flops 32 | bytes 256 | tf_op jit(solution)/shard_map/psum | solution.py:10
  261.9 0.6 multiply_reduce_fusion.1
  263.1 43.1 %all-reduce.3.cloned.1.call-done = f32[2880,32]{0,1:T(8,128)} async-done(((f32[2880,32]{0,1:T(8,128)}), f32[2880,32]{0,1:T(8,128)}) %all-reduce.3.cloned.1.call-update) | async-done | bytes 368656
  306.3 0.9 constant_dynamic-slice_fusion
  307.2 1.6 copy.52
  308.8 1.5 convolution_convert_fusion
  310.3 25.2 %reduce-scatter.4.cloned.1.call-done = f32[720,4]{1,0:T(8,128)} async-done(((f32[2880,4]{1,0:T(8,128)}), f32[720,4]{1,0:T(8,128)}) %reduce-scatter.4.cloned.1.call-update) | async-done | bytes 11536
  335.5 1.1 copy.53
  336.7 0.6 broadcast_multiply_fusion
  (38 shorter events, 1.6 us)
Async XLA Ops:
  7.2 209.1 %copy-start = (bf16[192,2880]{1,0:T(8,128)(2,1)S(1)}, bf16[192,2880]{1,0:T(8,128)(2,1)}, u32[]{:S(2)}) copy-start(bf16[192,2880]{1,0:T(8,128)(2,1)} %param.8) | copy-start | bytes 3317764
  14.2 7.5 %copy-start.3 = (s32[192,4]{0,1:T(4,128)S(1)}, s32[192,4]{0,1:T(4,128)}, u32[]{:S(2)}) copy-start(s32[192,4]{0,1:T(4,128)} %param.9) | copy-start | bytes 9220
  14.2 8.5 %copy-start.1 = (bf16[192,2880]{1,0:T(8,128)(2,1)S(1)}, bf16[192,2880]{1,0:T(8,128)(2,1)}, u32[]{:S(2)}) copy-start(bf16[192,2880]{1,0:T(8,128)(2,1)} %param.7) | copy-start | bytes 3317764
  14.2 8.5 %copy-start.2 = (bf16[2880,32]{0,1:T(8,128)(2,1)S(1)}, bf16[2880,32]{0,1:T(8,128)(2,1)}, u32[]{:S(2)}) copy-start(bf16[2880,32]{0,1:T(8,128)(2,1)} %param.11) | copy-start | bytes 552964
  14.2 8.5 %copy-start.4 = (f32[32]{0:T(128)S(1)}, f32[32]{0:T(128)}, u32[]{:S(2)}) copy-start(f32[32]{0:T(128)} %param.12) | copy-start | bytes 388
  14.2 172.5 %all-to-all-start = ((bf16[1,4,8,36,2880]{4,3,1,0,2:T(8,128)(2,1)}), bf16[1,4,8,36,2880]{4,3,1,0,2:T(8,128)(2,1)}, u32[]{:S(2)}, u32[]{:S(2)}) async-start(bf16[1,4,8,36,2880]{4,3,1,0,2:T(8,128)(2,1)} %copy.48), calls=%async_computation | async-start | bytes 15073280 | tf_op jit(solution)/shard_map/all_to_all | solution.py:35
  21.7 284.6 %all-reduce.3.cloned.1.call-start = ((), (), s32[]{:S(2)}) async-start(), calls=%async_computation.3 | async-start | bytes 753664
  216.2 10.8 %copy-start.5 = (u32[32]{0:T(128)S(1)}, u32[32]{0:T(128)}, u32[]{:S(2)}) copy-start(u32[32]{0:T(128)} %constant.70) | copy-start | bytes 388
  227.0 108.5 %reduce-scatter.4.cloned.1.call-start = ((), (), s32[]{:S(2)}) async-start(), calls=%async_computation.2 | async-start | bytes 1843200
Sparse Core Ops, SparseCore 0:
  227.1 79.0 all-reduce.2
  308.9 26.5 reduce-scatter.3
